TPU v7x, 256 devices: a whole 4x4x8 slice. The times are simulated.
256 devices in a mesh: rep: 8 (over x_lo, y), ep: 32 (over x_hi, z, core).
Axes of the slice: x: 4 (x_hi: 2, x_lo: 2; x = x_hi * 2 + x_lo), y: 4, z: 8, core: 2. Of those that a mesh axis runs over, the one named last changes fastest.
Arguments:
- hidden: bfloat16 [4, 8192, 2, 2048], P(None, ('rep', 'ep')), may hold values from -6 to 6
- out_grad: bfloat16 [4, 8192, 7168], P(None, ('rep', 'ep')), may hold values from -0.5 to 0.5
- route_weight: float32 [4, 8192, 2], P(None, ('rep', 'ep')), may hold values from 0.05 to 1
- expert_ids: int32 [4, 8192, 2], P(None, ('rep', 'ep')), may hold values from 0 to 31, as said below
Outputs:
- grad_down: bfloat16 [32, 2048, 7168], P('ep', None, 'rep')
- expert_load: float32 [32], replicated
Inputs may be any that keep to these rules, and one draw needn't show every extreme that they name: `expert_ids`: in each micro-batch the 32 tokens of one device (aligned blocks of 32 tokens) name no expert in more than 4 pairs, and some expert is named in exactly 4; the 2 experts of a token differ.
All inputs are finite; a program needn't handle non-finite values.
Results may differ from a plain program's by a relative error of at most 0.0049.
Values may be sent and summed in bfloat16 or wider, within the bound.
A program may use at most 192 MiB of HBM per device.

v0:
```python
import functools

import jax
import jax.numpy as jnp
from jax import lax
from jax.experimental import pallas as pl
from jax.experimental.pallas import tpu as pltpu
from jax.sharding import Mesh
from jax.sharding import PartitionSpec as P

REP_EP = ("rep_0", "rep_1", "ep_0", "ep_1", "ep_2")
EP = ("ep_0", "ep_1", "ep_2")
REP = ("rep_0", "rep_1")
MESH = pl.DeviceIdType.MESH
NX, NY, NZ, NC = 4, 4, 8, 2
NE = NZ * NC
NQ = NX * NY
NEAR = 5
CHUNKS = 4
ZC = [(1, 0), (7, 0), (1, 1), (7, 1), (2, 0), (6, 0), (2, 1), (6, 1), (3, 0), (5, 0), (3, 1), (5, 1), (4, 0), (4, 1), (0, 1)]
GROUP_DY = [0, 1, 3, 2]
ORDER = [
    ("hid", 0), ("routes", 0), ("raw", 0), ("hid", 1), ("turn", 0), ("raw", 1), ("far", 0), ("row", 0), ("hid", 2),
    ("raw", 2), ("turn", 1), ("far", 1), ("pack", 0), ("row", 1), ("relay", 0), ("hid", 3), ("raw", 3), ("turn", 2),
    ("far", 2), ("pack", 1), ("row", 2), ("relay", 1), ("turn", 3), ("far", 3), ("row", 3), ("pack", 2), ("relay", 2),
    ("pack", 3), ("relay", 3),
    ("mul", 0, 0, 4), ("mul", 1, 0, 4), ("mul", 2, 0, 4), ("mul", 3, 0, 4),
]


def kernel(hid_ref, slot_ref, meta_ref, og_ref, out_ref, load_ref,
           graw, meta, gnear, gfar, gall, hp, hz, hzt, ht, acc, cnt, cnt_all, cnt_x,
           s_send, s_meta, s_first, s_raw, s_gz, s_hz, s_hx, s_hy, s_cnt):
    cap, step = hp.shape[3], hp.shape[4]
    cols = graw.shape[5]
    toks = graw.shape[3] * graw.shape[4]
    pairs = hid_ref.shape[0]
    xlo, y = lax.axis_index("rep_0"), lax.axis_index("rep_1")
    xhi, z, core = lax.axis_index("ep_0"), lax.axis_index("ep_1"), lax.axis_index("ep_2")
    x = xhi * 2 + xlo

    def in_plane(dxl, dy):
        x2, y2 = lax.rem(xlo + dxl, 2), lax.rem(y + dy, NY)
        return x2, y2, {"rep_0": x2, "rep_1": y2}

    def along_x(dx):
        x2 = lax.rem(x + dx, NX)
        return x2 // 2, {"ep_0": x2 // 2, "rep_0": lax.rem(x2, 2)}

    def zc(dz, dc):
        z2, c2 = lax.rem(z + dz, NZ), lax.rem(core + dc, NC)
        return z2 * NC + c2, {"ep_1": z2, "ep_2": c2}

    def owner(dxh, dz, dc):
        h2, z2, c2 = lax.rem(xhi + dxh, 2), lax.rem(z + dz, NZ), lax.rem(core + dc, NC)
        return h2 * NC + c2, c2, {"ep_0": h2, "ep_1": z2, "ep_2": c2}

    def send(src, dst, send_sem, recv_sem, dev):
        pltpu.make_async_remote_copy(
            src_ref=src, dst_ref=dst, send_sem=s_send.at[send_sem], recv_sem=recv_sem, device_id=dev,
            device_id_type=MESH,
        ).start()

    def keep(src, dst, sem):
        pltpu.make_async_copy(src, dst, sem).start()

    def wait(ref, sem):
        pltpu.make_async_copy(ref, ref, sem).wait()

    barrier = pltpu.get_barrier_semaphore()
    partners = [in_plane(dxl, dy)[2] for dy in range(NY) for dxl in range(2) if dxl or dy]
    partners += [zc(dz, dc)[1] for dz, dc in ZC]
    partners += [{"ep_0": 1 - xhi, "rep_0": 1 - xlo}]
    partners += [owner(1, dz, dc)[2] for dz in (0, 1, 7, 2, 6) for dc in range(2)]
    for dev in partners:
        pl.semaphore_signal(barrier, inc=1, device_id=dev, device_id_type=MESH)
    pl.semaphore_wait(barrier, len(partners))

    toward = [(g, (NY - GROUP_DY[g]) % NY, dxl) for g in range(NY) for dxl in (1, 0)]
    for g, dy, dxl in toward:
        if dxl or dy:
            send(meta_ref, meta.at[2, g * 2 + xlo], 0, s_meta.at[2], in_plane(dxl, dy)[2])
    keep(meta_ref, meta.at[2, xlo], s_meta.at[2])
    for g, dy, dxl in toward:
        x2, y2, dev = in_plane(dxl, dy)
        piece = og_ref.at[:, :, pl.ds(pl.multiple_of((x2 * NY + y2) * cols, 128), cols)]
        if dxl or dy:
            send(piece, graw.at[g, 2, xlo], 2 if g else 1, s_first.at[g], dev)
        else:
            keep(piece, graw.at[g, 2, xlo], s_first.at[g])

    half = NE * cap
    for c in range(CHUNKS):
        for i in range(2):
            sel = jnp.where(
                lax.broadcasted_iota(jnp.int32, (half, pairs), 0) + i * half == slot_ref[...], 1.0, 0.0
            ).astype(jnp.bfloat16)
            packed = jnp.dot(sel, hid_ref[:, c * step:(c + 1) * step], preferred_element_type=jnp.float32)
            hp[c, i] = packed.astype(jnp.bfloat16).reshape(NE, cap, step)

    def hid(c):
        for dz, dc in ZC:
            e, dev = zc(dz, dc)
            send(hp.at[c, :, e], hz.at[c, :, core, (2 - dz) % NZ], 3 if dz else 4, s_hz.at[c], dev)
        keep(hp.at[c, :, z * NC + core], hz.at[c, :, core, 2], s_hz.at[c])

    eye = jnp.where(
        lax.broadcasted_iota(jnp.int32, (256, 256), 0) == lax.broadcasted_iota(jnp.int32, (256, 256), 1), 1.0, 0.0
    ).astype(jnp.bfloat16)

    def turn(c):
        wait(hz.at[c], s_hz.at[c])
        for i in range(2):
            for f in range(0, step, 256):
                block = hz[c, i, :, :, :, f:f + 256].reshape(half, 256)
                turned = lax.dot_general(eye, block, (((1,), (1,)), ((), ())), preferred_element_type=jnp.float32)
                hzt[c, i, f:f + 256, :] = turned.astype(jnp.bfloat16)
        for dx in (1, 3, 2):
            h2, dev = along_x(dx)
            send(hzt.at[c, h2], ht.at[x, c], 5, s_hx.at[c], dev)
        keep(hzt.at[c, xhi], ht.at[x, c], s_hx.at[c])

    up, down = in_plane(0, 1)[2], in_plane(0, 3)[2]

    def row(c):
        own = ht.at[pl.ds(0, NX), c]
        wait(own, s_hx.at[c])
        send(own, ht.at[pl.ds(2 * NX, NX), c], 6, s_hy.at[0, c], up)
        send(own, ht.at[pl.ds(NX, NX), c], 6, s_hy.at[1, c], down)

    def relay(c):
        wait(ht.at[pl.ds(2 * NX, NX), c], s_hy.at[0, c])
        send(ht.at[pl.ds(2 * NX, 2), c], ht.at[pl.ds(3 * NX, 2), c], 7, s_hy.at[2, c], up)
        wait(ht.at[pl.ds(NX, NX), c], s_hy.at[1, c])
        send(ht.at[pl.ds(NX + 2, 2), c], ht.at[pl.ds(3 * NX + 2, 2), c], 7, s_hy.at[3, c], down)

    def routes(_):
        wait(meta.at[2], s_meta.at[2])
        for dz, at in ((1, 1), (7, 3), (2, 0), (6, 4)):
            send(meta.at[2], meta.at[at], 8, s_meta.at[at], zc(dz, 0)[1])
        total = meta[2, 0]
        for q in range(1, 2 * NY):
            total = total + meta[2, q]
        cnt[...] = total

    plus, minus = zc(1, 0)[1], zc(7, 0)[1]

    def raw(g):
        wait(graw.at[g, 2], s_first.at[g])
        send(graw.at[g, 2], graw.at[g, 1], 9, s_raw.at[g, 1], plus)
        send(graw.at[g, 2], graw.at[g, 3], 9, s_raw.at[g, 3], minus)

    def far(g):
        wait(graw.at[g, 1], s_raw.at[g, 1])
        send(graw.at[g, 1], graw.at[g, 0], 9, s_raw.at[g, 0], plus)
        wait(graw.at[g, 3], s_raw.at[g, 3])
        send(graw.at[g, 3], graw.at[g, 4], 9, s_raw.at[g, 4], minus)

    chip_rows = 2 * NC * cap

    def slots_of(count, z1, h2, z2):
        r = lax.broadcasted_iota(jnp.int32, (count, toks), 0)
        gap = half - NC * cap
        near = r + jnp.where(r >= NC * cap, gap, 0) + z * (NC * cap)
        if count == chip_rows:
            return near.astype(jnp.float32)
        s = r - chip_rows
        beyond = s + jnp.where(s >= NC * cap, gap, 0) + z1 * (NC * cap)
        last = s - chip_rows + h2 * half + z2 * (NC * cap)
        return jnp.where(r < chip_rows, near, jnp.where(s < chip_rows, beyond, last)).astype(jnp.float32)

    def pack(g):
        if g == 0:
            for at in (0, 1, 3, 4):
                wait(meta.at[at], s_meta.at[at])
        wait(graw.at[g, 0], s_raw.at[g, 0])
        wait(graw.at[g, 4], s_raw.at[g, 4])

        @pl.loop(0, 2)
        def _(xl):
            for at in range(NEAR):
                if at == 0:
                    rows = slots_of(chip_rows * 5 // 2, lax.rem(z + 1, NZ), xhi, lax.rem(z + 2, NZ))
                elif at == NEAR - 1:
                    rows = slots_of(chip_rows * 5 // 2, lax.rem(z + 7, NZ), 1 - xhi, lax.rem(z + 6, NZ))
                else:
                    rows = slots_of(chip_rows, 0, 0, 0)
                info = meta[at, g * 2 + xl]
                first = rows == info[0:1, :]
                second = rows == info[1:2, :]
                weights = jnp.where(first, info[2:3, :], jnp.where(second, info[3:4, :], 0.0))
                weight = jnp.sum(weights, axis=1, keepdims=True)
                sel = jnp.where(first | second, 1.0, 0.0).astype(jnp.bfloat16)
                packed = jnp.dot(sel, graw[g, at, xl].reshape(toks, cols), preferred_element_type=jnp.float32) * weight
                packed = packed.astype(jnp.bfloat16)
                gnear[g, :, xl, at] = packed[:chip_rows].reshape(2 * NC, cap, cols)
                if at == 0 or at == NEAR - 1:
                    gfar[g, at // 4, :, xl] = packed[chip_rows:].reshape(3 * NC, cap, cols)

        here = pl.ds(g * NX + xhi * 2, 2)
        for side, dz, at in ((0, 1, 7), (1, 7, 5)):
            for dxh in range(2):
                for dc in range(2):
                    d, _, dev = owner(dxh, dz, dc)
                    send(gfar.at[g, side, d], gall.at[here, core, at], 10, s_gz.at[g], dev)
        for side, dz in ((0, 2), (1, 6)):
            for dc in range(2):
                _, c2, dev = owner(side, dz, dc)
                send(gfar.at[g, side, 2 * NC + c2], gall.at[here, core, 6], 10, s_gz.at[g], dev)
        for dxh, dc in ((1, 0), (1, 1), (0, 1)):
            d, _, dev = owner(dxh, 0, dc)
            send(gnear.at[g, d], gall.at[here, core, pl.ds(0, NEAR)], 11, s_gz.at[g], dev)
        keep(gnear.at[g, xhi * NC + core], gall.at[here, core, pl.ds(0, NEAR)], s_gz.at[g])
        if g == 0:
            me = z * NC + core
            for dz, dc in ZC:
                send(cnt, cnt_all.at[me], 12, s_cnt.at[0], zc(dz, dc)[1])
            keep(cnt, cnt_all.at[me], s_cnt.at[0])
        if g == 1:
            wait(cnt_all, s_cnt.at[0])
            loads = cnt_all[0]
            for e in range(1, NE):
                loads = loads + cnt_all[e]
            cnt_x[0] = loads
        if g == 2:
            send(cnt_x.at[0], cnt_x.at[1], 13, s_cnt.at[1], owner(1, 0, 0)[2])

    ready = set()

    def mul(g, c0, c1):
        if g not in ready:
            ready.add(g)
            wait(gall.at[pl.ds(g * NX, NX)], s_gz.at[g])
        if g == NY - 1:
            for c in range(c0, c1):
                wait(ht.at[pl.ds(3 * NX, 2), c], s_hy.at[2, c])
                wait(ht.at[pl.ds(3 * NX + 2, 2), c], s_hy.at[3, c])

        @pl.loop(c0, c1)
        def _(c):
            at = pl.ds(pl.multiple_of(c * step, step), step)
            part = None
            for xs in range(NX):
                q = g * NX + xs
                term = jnp.dot(ht[q, c], gall[q].reshape(half, cols), preferred_element_type=jnp.float32)
                part = term if part is None else part + term
            if g == 0:
                acc[at, :] = part
            elif g < NY - 1:
                acc[at, :] += part
            else:
                out_ref[0, at, :] = (acc[at, :] + part).astype(out_ref.dtype)

    steps = dict(hid=hid, routes=routes, raw=raw, turn=turn, far=far, row=row, relay=relay, pack=pack, mul=mul)
    for name, *which in ORDER:
        steps[name](*which)

    wait(cnt_x.at[1], s_cnt.at[1])
    load_ref[...] = cnt_x[0] + cnt_x[1]

    sent = (
        meta.at[2, pl.ds(0, 7)], graw.at[0, 2, 0], graw.at[pl.ds(1, 3), 2], hz.at[:, :, :, pl.ds(0, 7)],
        hz.at[:, :, 0, 0], ht.at[pl.ds(0, 3)], ht.at[pl.ds(0, 2 * NX)], ht.at[pl.ds(0, NX)],
        meta.at[pl.ds(0, 4)], graw.at[:, pl.ds(0, 4)], gfar, gnear.at[:, pl.ds(0, 3)],
        cnt_all.at[pl.ds(0, NE - 1)], cnt_x.at[0],
    )
    for i, ref in enumerate(sent):
        wait(ref, s_send.at[i])


def body(hidden, out_grad, route_weight, expert_ids):
    micro, tokens, picks, ff = hidden.shape
    width = out_grad.shape[2]
    experts = lax.axis_size(EP)
    replicas = lax.axis_size(REP)
    cols = width // replicas
    limit = 2 * tokens * picks // experts
    cap = micro * limit
    toks = micro * tokens
    ids = expert_ids.reshape(micro, tokens * picks)
    order = jnp.arange(tokens * picks, dtype=jnp.int32)
    earlier = (ids[:, :, None] == ids[:, None, :]) & (order[None, None, :] < order[None, :, None])
    position = jnp.sum(earlier.astype(jnp.int32), axis=2)
    slot = ids * cap + jnp.arange(micro, dtype=jnp.int32)[:, None] * limit + position
    by_token = slot.reshape(toks, picks).T.astype(jnp.float32)
    weights = route_weight.reshape(toks, picks).T
    tally = jnp.sum(
        (expert_ids.reshape(toks * picks)[None, :] == jnp.arange(toks, dtype=jnp.int32)[:, None]).astype(jnp.float32),
        axis=1,
    )
    meta = jnp.concatenate([by_token, weights, tally[None, :], jnp.zeros((3, toks), jnp.float32)], axis=0)
    vmem = pl.BlockSpec(memory_space=pltpu.VMEM)
    bf16 = jnp.bfloat16
    dma = pltpu.SemaphoreType.DMA
    grad, load = pl.pallas_call(
        kernel,
        out_shape=(
            jax.ShapeDtypeStruct((1, ff, cols), bf16),
            jax.ShapeDtypeStruct((8, toks), jnp.float32),
        ),
        in_specs=[vmem, vmem, vmem, pl.BlockSpec(memory_space=pl.ANY)],
        out_specs=(vmem, vmem),
        scratch_shapes=[
            pltpu.VMEM((NY, NEAR, 2, micro, tokens, cols), bf16),
            pltpu.VMEM((NEAR, 2 * NY, 8, toks), jnp.float32),
            pltpu.VMEM((NY, 2 * NC, 2, NEAR, cap, cols), bf16),
            pltpu.VMEM((NY, 2, 3 * NC, 2, cap, cols), bf16),
            pltpu.VMEM((NQ, NC, NZ, cap, cols), bf16),
            pltpu.VMEM((CHUNKS, 2, NE, cap, ff // CHUNKS), bf16),
            pltpu.VMEM((CHUNKS, 2, NC, NZ, cap, ff // CHUNKS), bf16),
            pltpu.VMEM((CHUNKS, 2, ff // CHUNKS, NE * cap), bf16),
            pltpu.VMEM((NQ, CHUNKS, ff // CHUNKS, NE * cap), bf16),
            pltpu.VMEM((ff, cols), jnp.float32),
            pltpu.VMEM((8, toks), jnp.float32),
            pltpu.VMEM((NE, 8, toks), jnp.float32),
            pltpu.VMEM((2, 8, toks), jnp.float32),
            dma((14,)),
            dma((NEAR,)),
            dma((NY,)),
            dma((NY, NEAR)),
            dma((NY,)),
            dma((CHUNKS,)),
            dma((CHUNKS,)),
            dma((4, CHUNKS)),
            dma((2,)),
        ],
        compiler_params=pltpu.CompilerParams(
            collective_id=0, has_side_effects=True, vmem_limit_bytes=67_000_000 // 1024 * 1024
        ),
    )(hidden.reshape(toks * picks, ff), slot.reshape(1, toks * picks), meta, out_grad)
    expert_load = load[4, :experts] / float(micro * tokens * replicas * picks)
    return grad, expert_load


def solution(mesh):
    finer = Mesh(mesh.devices.reshape(2, 4, 2, 8, 2), REP_EP)
    placed = (
        P(None, REP_EP, None, None),
        P(None, REP_EP, None),
        P(None, REP_EP, None),
        P(None, REP_EP, None),
    )
    return jax.shard_map(
        body, mesh=finer, in_specs=placed, out_specs=(P(EP, None, REP), P()), check_vma=False
    )
```

profile of v0, /device:TPU:1, one launch (start us, length us, event | category | flops | bytes accessed | tf_op | source)
XLA Modules:
  0.0 217.0 jit_solution(13849207131833590668)
XLA Ops:
  0.6 0.1 pad.3.clone
  0.7 0.1 add.43
  0.8 0.1 add.44
  0.9 0.1 add.39
  0.9 0.1 add.40
  1.0 0.7 broadcast_multiply_fusion
  1.7 0.1 mul.34
  1.8 0.7 copy.23
  2.5 0.1 reshape.78
  2.6 0.8 copy.18
  3.4 0.1 copy.19
  3.5 0.2 convert_reduce_fusion.1
  3.7 0.1 reduce_sum.23
  3.8 0.1 copy.17
  3.9 0.1 mul.32
  4.0 0.6 add_add_fusion.slot_ref
  4.6 0.1 reduce_sum.24
  4.7 0.1 copy.22
  4.8 0.8 copy.24
  5.6 0.1 eq.34
  5.8 0.1 convert_reduce_fusion
  5.9 0.7 maximum_maximum_fusion.meta_ref
  6.5 2.2 %reshape.77.hid_ref = bf16[256,2048]{1,0:T(8,128)(2,1)} reshape(bf16[4,32,2,2048]{3,2,1,0:T(2,128)(2,1)} %param.4) | data formatting | bytes 2097152 | tf_op jit(solution)/shard_map/reshape | solution.py:330
  8.8 202.8 %shard_map.59 = (bf16[1,2048,896]{2,1,0:T(8,128)(2,1)}, f32[8,128]{1,0:T(8,128)}) custom-call(bf16[256,2048]{1,0:T(8,128)(2,1)} %reshape.77.hid_ref, s32[1,256]{1,0:T(1,128)} %add_add_fusion.slot_ref, f32[8,128]{1,0:T(8,128)} %maximum_maximum_fusion.meta_ref, bf16[4,32,7168]{2,1,0:T(8,128)(2,1)} %og_ref.1), custom_call_target="tpu_custom_call" | custom-call | tf_op jit(solution)/shard_map/pallas_call | solution.py:295
  211.6 1.2 multiply_bitcast_fusion
  212.8 4.2 %copy.26 = bf16[1,2048,896]{2,1,0:T(8,128)(2,1)} copy(bf16[1,2048,896]{2,1,0:T(8,128)(2,1)} %get-tuple-element.8) | data formatting | bytes 7340032
  (5 shorter events, 0.0 us)
where the time goes:
time: 217 us
  Pallas kernels  203 us (94%)
  local copies, waits for them, and re-layouts  9.96 us (5%)
  other arithmetic  3.51 us (2%)
    pallas_call x1, Pallas kernels, body(): pl.pallas_call(kernel, out_shape=(jax.ShapeDtypeStruct((1, ff, cols), bf1...  203 us
    unnamed x4, local copies, waits for them, and re-layouts  6.45 us

commit v1 on v0

--- a/solution.py
+++ b/solution.py
@@ -16,15 +16,19 @@
 NE = NZ * NC
 NQ = NX * NY
 NEAR = 5
-CHUNKS = 4
+CHUNKS = 8
 ZC = [(1, 0), (7, 0), (1, 1), (7, 1), (2, 0), (6, 0), (2, 1), (6, 1), (3, 0), (5, 0), (3, 1), (5, 1), (4, 0), (4, 1), (0, 1)]
 GROUP_DY = [0, 1, 3, 2]
 ORDER = [
-    ("hid", 0), ("routes", 0), ("raw", 0), ("hid", 1), ("turn", 0), ("raw", 1), ("far", 0), ("row", 0), ("hid", 2),
-    ("raw", 2), ("turn", 1), ("far", 1), ("pack", 0), ("row", 1), ("relay", 0), ("hid", 3), ("raw", 3), ("turn", 2),
-    ("far", 2), ("pack", 1), ("row", 2), ("relay", 1), ("turn", 3), ("far", 3), ("row", 3), ("pack", 2), ("relay", 2),
-    ("pack", 3), ("relay", 3),
-    ("mul", 0, 0, 4), ("mul", 1, 0, 4), ("mul", 2, 0, 4), ("mul", 3, 0, 4),
+    ("fill", 0), ("hid", 0), ("fill", 3), ("fill", 5), ("fill", 4), ("fill", 6), ("hid", 5), ("turn", 0), ("fill", 2),
+    ("routes", 0), ("hid", 4), ("hid", 6), ("turn", 5), ("late", 0), ("hid", 3), ("fill", 7), ("row", 0), ("hid", 7),
+    ("count", 0), ("fill", 1), ("hid", 2), ("row", 5), ("hid", 1), ("turn", 3), ("turn", 7), ("turn", 4), ("raw", 1),
+    ("relay", 0), ("raw", 0), ("turn", 6), ("raw", 3), ("row", 3), ("row", 6), ("turn", 2), ("turn", 1), ("far", 0),
+    ("raw", 2), ("row", 7), ("near", 0), ("relay", 6), ("pack", 0), ("far", 1), ("row", 1), ("near", 1), ("far", 2),
+    ("far", 3), ("row", 4), ("near", 2), ("row", 2), ("relay", 5), ("mul", 0, 0, 4), ("relay", 1), ("near", 3),
+    ("mul", 0, 4, 8), ("pack", 1), ("pack", 2), ("pack", 3), ("relay", 2), ("relay", 3), ("relay", 7), ("relay", 4),
+    ("mul", 1, 4, 8), ("count", 1), ("mul", 2, 4, 8), ("mul", 1, 0, 4), ("mul", 2, 0, 4), ("count", 2),
+    ("mul", 3, 0, 4), ("mul", 3, 4, 8),
 ]
 
 
@@ -81,7 +85,8 @@
         if dxl or dy:
             send(meta_ref, meta.at[2, g * 2 + xlo], 0, s_meta.at[2], in_plane(dxl, dy)[2])
     keep(meta_ref, meta.at[2, xlo], s_meta.at[2])
-    for g, dy, dxl in toward:
+
+    def first(g, dy, dxl):
         x2, y2, dev = in_plane(dxl, dy)
         piece = og_ref.at[:, :, pl.ds(pl.multiple_of((x2 * NY + y2) * cols, 128), cols)]
         if dxl or dy:
@@ -89,8 +94,18 @@
         else:
             keep(piece, graw.at[g, 2, xlo], s_first.at[g])
 
+    for which in toward:
+        if which[0] < 2 or not which[2]:
+            first(*which)
+
+    def late(_):
+        for which in toward:
+            if which[0] >= 2 and which[2]:
+                first(*which)
+
     half = NE * cap
-    for c in range(CHUNKS):
+
+    def fill(c):
         for i in range(2):
             sel = jnp.where(
                 lax.broadcasted_iota(jnp.int32, (half, pairs), 0) + i * half == slot_ref[...], 1.0, 0.0
@@ -169,16 +184,10 @@
         last = s - chip_rows + h2 * half + z2 * (NC * cap)
         return jnp.where(r < chip_rows, near, jnp.where(s < chip_rows, beyond, last)).astype(jnp.float32)
 
-    def pack(g):
-        if g == 0:
-            for at in (0, 1, 3, 4):
-                wait(meta.at[at], s_meta.at[at])
-        wait(graw.at[g, 0], s_raw.at[g, 0])
-        wait(graw.at[g, 4], s_raw.at[g, 4])
-
+    def into_slots(g, sources):
         @pl.loop(0, 2)
         def _(xl):
-            for at in range(NEAR):
+            for at in sources:
                 if at == 0:
                     rows = slots_of(chip_rows * 5 // 2, lax.rem(z + 1, NZ), xhi, lax.rem(z + 2, NZ))
                 elif at == NEAR - 1:
@@ -197,6 +206,31 @@
                 if at == 0 or at == NEAR - 1:
                     gfar[g, at // 4, :, xl] = packed[chip_rows:].reshape(3 * NC, cap, cols)
 
+    def to_owners(g, first, count):
+        here, some = pl.ds(g * NX + xhi * 2, 2), pl.ds(first, count)
+        for dxh, dc in ((1, 0), (1, 1), (0, 1)):
+            d, _, dev = owner(dxh, 0, dc)
+            send(gnear.at[g, d, :, some], gall.at[here, core, some], 11, s_gz.at[g], dev)
+        keep(gnear.at[g, xhi * NC + core, :, some], gall.at[here, core, some], s_gz.at[g])
+
+    seen = set()
+
+    def known(offsets):
+        for at in offsets:
+            if at not in seen:
+                seen.add(at)
+                wait(meta.at[at], s_meta.at[at])
+
+    def near(g):
+        known((1, 3))
+        into_slots(g, (1, 2, 3))
+        to_owners(g, 1, 3)
+
+    def pack(g):
+        known((0, 4))
+        wait(graw.at[g, 0], s_raw.at[g, 0])
+        wait(graw.at[g, 4], s_raw.at[g, 4])
+        into_slots(g, (0, 4))
         here = pl.ds(g * NX + xhi * 2, 2)
         for side, dz, at in ((0, 1, 7), (1, 7, 5)):
             for dxh in range(2):
@@ -207,23 +241,24 @@
             for dc in range(2):
                 _, c2, dev = owner(side, dz, dc)
                 send(gfar.at[g, side, 2 * NC + c2], gall.at[here, core, 6], 10, s_gz.at[g], dev)
-        for dxh, dc in ((1, 0), (1, 1), (0, 1)):
-            d, _, dev = owner(dxh, 0, dc)
-            send(gnear.at[g, d], gall.at[here, core, pl.ds(0, NEAR)], 11, s_gz.at[g], dev)
-        keep(gnear.at[g, xhi * NC + core], gall.at[here, core, pl.ds(0, NEAR)], s_gz.at[g])
-        if g == 0:
+        to_owners(g, 0, 1)
+        to_owners(g, 4, 1)
+
+    def count(part):
+        if part == 0:
             me = z * NC + core
             for dz, dc in ZC:
                 send(cnt, cnt_all.at[me], 12, s_cnt.at[0], zc(dz, dc)[1])
             keep(cnt, cnt_all.at[me], s_cnt.at[0])
-        if g == 1:
-            wait(cnt_all, s_cnt.at[0])
-            loads = cnt_all[0]
-            for e in range(1, NE):
-                loads = loads + cnt_all[e]
-            cnt_x[0] = loads
-        if g == 2:
+            return
+        if part == 2:
             send(cnt_x.at[0], cnt_x.at[1], 13, s_cnt.at[1], owner(1, 0, 0)[2])
+            return
+        wait(cnt_all, s_cnt.at[0])
+        loads = cnt_all[0]
+        for e in range(1, NE):
+            loads = loads + cnt_all[e]
+        cnt_x[0] = loads
 
     ready = set()
 
@@ -251,7 +286,7 @@
             else:
                 out_ref[0, at, :] = (acc[at, :] + part).astype(out_ref.dtype)
 
-    steps = dict(hid=hid, routes=routes, raw=raw, turn=turn, far=far, row=row, relay=relay, pack=pack, mul=mul)
+    steps = dict(fill=fill, late=late, near=near, count=count, hid=hid, routes=routes, raw=raw, turn=turn, far=far, row=row, relay=relay, pack=pack, mul=mul)
     for name, *which in ORDER:
         steps[name](*which)
 

time: 217 us -> 208 us (0.959); the launches traced: 217 us -> 205 us
  Pallas kernels: 203 us -> 191 us
    pallas_call x1, Pallas kernels: 203 us -> 191 us  [body(): pl.pallas_call(kernel, out_shape=(jax.ShapeDtypeStruct((1, ff, cols), bf1...]
where the time goes in v1:
time: 208 us; the launch traced here: 205 us
  Pallas kernels  191 us (92%)
  local copies, waits for them, and re-layouts  9.96 us (5%)
  other arithmetic  3.51 us (2%)
    pallas_call x1, Pallas kernels, body(): pl.pallas_call(kernel, out_shape=(jax.ShapeDtypeStruct((1, ff, cols), bf1...  191 us
    unnamed x4, local copies, waits for them, and re-layouts  6.45 us

profile of v1, /device:TPU:1, one launch (start us, length us, event | category | flops | bytes accessed | tf_op | source)
XLA Modules:
  0.0 205.1 jit_solution(18428264418046036567)
XLA Ops:
  0.6 0.1 pad.3.clone
  0.7 0.1 add.43
  0.8 0.1 add.44
  0.9 0.1 add.39
  0.9 0.1 add.40
  1.0 0.7 broadcast_multiply_fusion
  1.7 0.1 mul.34
  1.8 0.7 copy.23
  2.5 0.1 reshape.78
  2.6 0.8 copy.18
  3.4 0.1 copy.19
  3.5 0.2 convert_reduce_fusion.1
  3.7 0.1 reduce_sum.23
  3.8 0.1 copy.17
  3.9 0.1 mul.32
  4.0 0.6 add_add_fusion.slot_ref
  4.6 0.1 reduce_sum.24
  4.7 0.1 copy.22
  4.8 0.8 copy.24
  5.6 0.1 eq.34
  5.8 0.1 convert_reduce_fusion
  5.9 0.7 maximum_maximum_fusion.meta_ref
  6.5 2.2 %reshape.77.hid_ref = bf16[256,2048]{1,0:T(8,128)(2,1)} reshape(bf16[4,32,2,2048]{3,2,1,0:T(2,128)(2,1)} %param.4) | data formatting | bytes 2097152 | tf_op jit(solution)/shard_map/reshape | solution.py:365
  8.8 191.0 %shard_map.59 = (bf16[1,2048,896]{2,1,0:T(8,128)(2,1)}, f32[8,128]{1,0:T(8,128)}) custom-call(bf16[256,2048]{1,0:T(8,128)(2,1)} %reshape.77.hid_ref, s32[1,256]{1,0:T(1,128)} %add_add_fusion.slot_ref, f32[8,128]{1,0:T(8,128)} %maximum_maximum_fusion.meta_ref, bf16[4,32,7168]{2,1,0:T(8,128)(2,1)} %og_ref.1), custom_call_target="tpu_custom_call" | custom-call | tf_op jit(solution)/shard_map/pallas_call | solution.py:330
  199.8 1.2 multiply_bitcast_fusion
  201.0 4.2 %copy.26 = bf16[1,2048,896]{2,1,0:T(8,128)(2,1)} copy(bf16[1,2048,896]{2,1,0:T(8,128)(2,1)} %get-tuple-element.8) | data formatting | bytes 7340032
  (5 shorter events, 0.0 us)

commit v2 on v1

--- a/solution.py
+++ b/solution.py
@@ -19,26 +19,31 @@
 CHUNKS = 8
 ZC = [(1, 0), (7, 0), (1, 1), (7, 1), (2, 0), (6, 0), (2, 1), (6, 1), (3, 0), (5, 0), (3, 1), (5, 1), (4, 0), (4, 1), (0, 1)]
 GROUP_DY = [0, 1, 3, 2]
+EARLY = [
+    ("fill", 0), ("fill", 1), ("fill", 2), ("fill", 3), ("fill", 4), ("fill", 5), ("fill", 6), ("fill", 7),
+]
 ORDER = [
-    ("fill", 0), ("hid", 0), ("fill", 3), ("fill", 5), ("fill", 4), ("fill", 6), ("hid", 5), ("turn", 0), ("fill", 2),
-    ("routes", 0), ("hid", 4), ("hid", 6), ("turn", 5), ("late", 0), ("hid", 3), ("fill", 7), ("row", 0), ("hid", 7),
-    ("count", 0), ("fill", 1), ("hid", 2), ("row", 5), ("hid", 1), ("turn", 3), ("turn", 7), ("turn", 4), ("raw", 1),
-    ("relay", 0), ("raw", 0), ("turn", 6), ("raw", 3), ("row", 3), ("row", 6), ("turn", 2), ("turn", 1), ("far", 0),
-    ("raw", 2), ("row", 7), ("near", 0), ("relay", 6), ("pack", 0), ("far", 1), ("row", 1), ("near", 1), ("far", 2),
-    ("far", 3), ("row", 4), ("near", 2), ("row", 2), ("relay", 5), ("mul", 0, 0, 4), ("relay", 1), ("near", 3),
-    ("mul", 0, 4, 8), ("pack", 1), ("pack", 2), ("pack", 3), ("relay", 2), ("relay", 3), ("relay", 7), ("relay", 4),
-    ("mul", 1, 4, 8), ("count", 1), ("mul", 2, 4, 8), ("mul", 1, 0, 4), ("mul", 2, 0, 4), ("count", 2),
+    ("hid", 0), ("hid", 5), ("turn", 0), ("routes", 0), ("hid", 4), ("hid", 6), ("turn", 5), ("late", 0), ("hid", 3),
+    ("row", 0), ("hid", 7), ("count", 0), ("hid", 2), ("row", 5), ("hid", 1), ("turn", 3), ("turn", 7), ("turn", 4),
+    ("raw", 1), ("relay", 0), ("raw", 0), ("turn", 6), ("raw", 3), ("row", 3), ("row", 6), ("turn", 2), ("turn", 1),
+    ("far", 0), ("raw", 2), ("row", 7), ("near", 0), ("relay", 6), ("pack", 0), ("far", 1), ("row", 1), ("near", 1),
+    ("far", 2), ("far", 3), ("row", 4), ("near", 2), ("row", 2), ("relay", 5), ("mul", 0, 0, 4), ("relay", 1),
+    ("near", 3), ("mul", 0, 4, 8), ("pack", 1), ("pack", 2), ("pack", 3), ("relay", 2), ("relay", 3), ("relay", 7),
+    ("relay", 4), ("mul", 1, 4, 8), ("count", 1), ("mul", 2, 4, 8), ("mul", 1, 0, 4), ("mul", 2, 0, 4), ("count", 2),
     ("mul", 3, 0, 4), ("mul", 3, 4, 8),
 ]
 
 
-def kernel(hid_ref, slot_ref, meta_ref, og_ref, out_ref, load_ref,
-           graw, meta, gnear, gfar, gall, hp, hz, hzt, ht, acc, cnt, cnt_all, cnt_x,
+def kernel(limit, total_pairs, hid_ref, ids_ref, weight_ref, og_ref, out_ref, load_ref,
+           meta_ref, pair_slot, graw, meta, gnear, gfar, gall, hp, hz, hzt, ht, acc, cnt, cnt_all, cnt_x,
            s_send, s_meta, s_first, s_raw, s_gz, s_hz, s_hx, s_hy, s_cnt):
     cap, step = hp.shape[3], hp.shape[4]
     cols = graw.shape[5]
     toks = graw.shape[3] * graw.shape[4]
-    pairs = hid_ref.shape[0]
+    micro, tokens, picks = hid_ref.shape[:3]
+    pairs = toks * picks
+    half = NE * cap
+    f32, bf16, i32 = jnp.float32, jnp.bfloat16, jnp.int32
     xlo, y = lax.axis_index("rep_0"), lax.axis_index("rep_1")
     xhi, z, core = lax.axis_index("ep_0"), lax.axis_index("ep_1"), lax.axis_index("ep_2")
     x = xhi * 2 + xlo
@@ -78,6 +83,59 @@
     partners += [owner(1, dz, dc)[2] for dz in (0, 1, 7, 2, 6) for dc in range(2)]
     for dev in partners:
         pl.semaphore_signal(barrier, inc=1, device_id=dev, device_id_type=MESH)
+
+    def across(ref, k):
+        return jnp.concatenate([ref[m, k:k + 1, :] for m in range(micro)], axis=1)
+
+    def square(rows):
+        return lax.broadcasted_iota(i32, (rows, toks), 0), lax.broadcasted_iota(i32, (rows, toks), 1)
+
+    down_at, along_at = square(toks)
+    same = down_at // tokens == along_at // tokens
+    block = jnp.where(same, 1.0, 0.0).astype(bf16)
+    before = jnp.where(same & (down_at < along_at), 1.0, 0.0).astype(bf16)
+    ids = [across(ids_ref, k) for k in range(picks)]
+    hits = [jnp.where(down_at == e, 1.0, 0.0).astype(bf16) for e in ids]
+    lane_micro = (lax.broadcasted_iota(i32, (1, toks), 1) // tokens).astype(f32)
+    within, passed = [], None
+    for hit in hits:
+        earlier = jnp.dot(hit, before, preferred_element_type=f32)
+        if passed is not None:
+            earlier = earlier + jnp.dot(passed, block, preferred_element_type=f32)
+        place = jnp.sum(hit.astype(f32) * earlier, axis=0, keepdims=True)
+        within.append(lane_micro * limit + place)
+        passed = hit if passed is None else passed + hit
+    tally = lax.dot_general(
+        jnp.ones((8, toks), bf16), passed, (((1,), (1,)), ((), ())), preferred_element_type=f32
+    )[0:1, :]
+    rows = [ids[k].astype(f32) * cap + within[k] for k in range(picks)]
+    rows += [across(weight_ref, k) for k in range(picks)] + [tally]
+    line = lax.broadcasted_iota(i32, (8, toks), 0)
+    own_meta = jnp.zeros((8, toks), f32)
+    for i, row_of in enumerate(rows):
+        own_meta = jnp.where(line == i, row_of, own_meta)
+    meta_ref[...] = own_meta
+    spread = jnp.zeros((8, pairs), f32)
+    eight = lax.broadcasted_iota(i32, (8, toks), 0)
+    for k in range(picks):
+        put = jnp.where(
+            lax.broadcasted_iota(i32, (toks, pairs), 1) == lax.broadcasted_iota(i32, (toks, pairs), 0) * picks + k, 1.0, 0.0
+        ).astype(bf16)
+        both = jnp.where(eight == 0, ids[k].astype(f32), within[k]).astype(bf16)
+        spread = spread + jnp.dot(both, put, preferred_element_type=f32)
+    pair_slot[...] = (spread[0:1, :] * cap + spread[1:2, :]).astype(i32)
+
+    def fill(c):
+        rows_here = hid_ref[:, :, :, c * step:(c + 1) * step].reshape(pairs, step)
+        for i in range(2):
+            sel = jnp.where(
+                lax.broadcasted_iota(i32, (half, pairs), 0) + i * half == pair_slot[...], 1.0, 0.0
+            ).astype(bf16)
+            packed = jnp.dot(sel, rows_here, preferred_element_type=f32)
+            hp[c, i] = packed.astype(bf16).reshape(NE, cap, step)
+
+    for name, *which in EARLY:
+        fill(*which)
     pl.semaphore_wait(barrier, len(partners))
 
     toward = [(g, (NY - GROUP_DY[g]) % NY, dxl) for g in range(NY) for dxl in (1, 0)]
@@ -102,16 +160,6 @@
         for which in toward:
             if which[0] >= 2 and which[2]:
                 first(*which)
-
-    half = NE * cap
-
-    def fill(c):
-        for i in range(2):
-            sel = jnp.where(
-                lax.broadcasted_iota(jnp.int32, (half, pairs), 0) + i * half == slot_ref[...], 1.0, 0.0
-            ).astype(jnp.bfloat16)
-            packed = jnp.dot(sel, hid_ref[:, c * step:(c + 1) * step], preferred_element_type=jnp.float32)
-            hp[c, i] = packed.astype(jnp.bfloat16).reshape(NE, cap, step)
 
     def hid(c):
         for dz, dc in ZC:
@@ -286,12 +334,12 @@
             else:
                 out_ref[0, at, :] = (acc[at, :] + part).astype(out_ref.dtype)
 
-    steps = dict(fill=fill, late=late, near=near, count=count, hid=hid, routes=routes, raw=raw, turn=turn, far=far, row=row, relay=relay, pack=pack, mul=mul)
+    steps = dict(late=late, near=near, count=count, hid=hid, routes=routes, raw=raw, turn=turn, far=far, row=row, relay=relay, pack=pack, mul=mul)
     for name, *which in ORDER:
         steps[name](*which)
 
     wait(cnt_x.at[1], s_cnt.at[1])
-    load_ref[...] = cnt_x[0] + cnt_x[1]
+    load_ref[...] = ((cnt_x[0, 4:5, :] + cnt_x[1, 4:5, :]) / total_pairs)[0, :load_ref.shape[0]]
 
     sent = (
         meta.at[2, pl.ds(0, 7)], graw.at[0, 2, 0], graw.at[pl.ds(1, 3), 2], hz.at[:, :, :, pl.ds(0, 7)],
@@ -312,30 +360,20 @@
     limit = 2 * tokens * picks // experts
     cap = micro * limit
     toks = micro * tokens
-    ids = expert_ids.reshape(micro, tokens * picks)
-    order = jnp.arange(tokens * picks, dtype=jnp.int32)
-    earlier = (ids[:, :, None] == ids[:, None, :]) & (order[None, None, :] < order[None, :, None])
-    position = jnp.sum(earlier.astype(jnp.int32), axis=2)
-    slot = ids * cap + jnp.arange(micro, dtype=jnp.int32)[:, None] * limit + position
-    by_token = slot.reshape(toks, picks).T.astype(jnp.float32)
-    weights = route_weight.reshape(toks, picks).T
-    tally = jnp.sum(
-        (expert_ids.reshape(toks * picks)[None, :] == jnp.arange(toks, dtype=jnp.int32)[:, None]).astype(jnp.float32),
-        axis=1,
-    )
-    meta = jnp.concatenate([by_token, weights, tally[None, :], jnp.zeros((3, toks), jnp.float32)], axis=0)
     vmem = pl.BlockSpec(memory_space=pltpu.VMEM)
     bf16 = jnp.bfloat16
     dma = pltpu.SemaphoreType.DMA
     grad, load = pl.pallas_call(
-        kernel,
+        functools.partial(kernel, limit, float(micro * tokens * replicas * picks)),
         out_shape=(
-            jax.ShapeDtypeStruct((1, ff, cols), bf16),
-            jax.ShapeDtypeStruct((8, toks), jnp.float32),
+            pltpu.VMEM((1, ff, cols), bf16),
+            pltpu.VMEM((experts,), jnp.float32),
         ),
         in_specs=[vmem, vmem, vmem, pl.BlockSpec(memory_space=pl.ANY)],
         out_specs=(vmem, vmem),
         scratch_shapes=[
+            pltpu.VMEM((8, toks), jnp.float32),
+            pltpu.VMEM((1, toks * picks), jnp.int32),
             pltpu.VMEM((NY, NEAR, 2, micro, tokens, cols), bf16),
             pltpu.VMEM((NEAR, 2 * NY, 8, toks), jnp.float32),
             pltpu.VMEM((NY, 2 * NC, 2, NEAR, cap, cols), bf16),
@@ -360,11 +398,10 @@
             dma((2,)),
         ],
         compiler_params=pltpu.CompilerParams(
-            collective_id=0, has_side_effects=True, vmem_limit_bytes=67_000_000 // 1024 * 1024
+            collective_id=0, has_side_effects=True, vmem_limit_bytes=62_000_000 // 1024 * 1024
         ),
-    )(hidden.reshape(toks * picks, ff), slot.reshape(1, toks * picks), meta, out_grad)
-    expert_load = load[4, :experts] / float(micro * tokens * replicas * picks)
-    return grad, expert_load
+    )(hidden, expert_ids.transpose(0, 2, 1), route_weight.transpose(0, 2, 1), out_grad)
+    return grad, load
 
 
 def solution(mesh):

time: 208 us -> 194 us (0.933)
  local copies, waits for them, and re-layouts: 9.96 us -> 2.35 us
  other arithmetic: 3.51 us -> 0 us
    unnamed x4 -> x2, local copies, waits for them, and re-layouts: 6.45 us -> 2.35 us
    reshape x2 -> x0, local copies, waits for them, and re-layouts: 2.33 us -> none  [the longest x1 2.24 us: body(): hidden.reshape(toks * picks, ff)]
where the time goes in v2:
time: 194 us; the launch traced here: 193 us
  Pallas kernels  190 us (98%)
  local copies, waits for them, and re-layouts  2.35 us (1%)
    pallas_call x1, Pallas kernels, body(): pl.pallas_call(functools.partial(kernel, limit, float(micro * tokens * re...  190 us

profile of v2, /device:TPU:1, one launch (start us, length us, event | category | flops | bytes accessed | tf_op | source)
XLA Modules:
  0.0 192.5 jit_solution(13163971920648449666)
XLA Ops:
  0.6 189.5 %shard_map.59 = (bf16[1,2048,896]{2,1,0:T(8,128)(2,1)S(1)}, f32[32]{0:T(128)S(1)}) custom-call(bf16[4,32,2,2048]{3,2,1,0:T(2,128)(2,1)} %hid_ref.1, s32[4,2,32]{2,1,0:T(2,128)} %bitcast.2, f32[4,2,32]{2,1,0:T(2,128)} %bitcast.3, bf16[4,32,7168]{2,1,0:T(8,128)(2,1)} %og_ref.1), custom_call_target="tpu_custom_call" | custom-call | tf_op jit(solution)/shard_map/pallas_call | solution.py:366
  190.2 1.8 copy.8
  192.0 0.5 copy.9

commit v3 on v2

--- a/solution.py
+++ b/solution.py
@@ -19,24 +19,24 @@
 CHUNKS = 8
 ZC = [(1, 0), (7, 0), (1, 1), (7, 1), (2, 0), (6, 0), (2, 1), (6, 1), (3, 0), (5, 0), (3, 1), (5, 1), (4, 0), (4, 1), (0, 1)]
 GROUP_DY = [0, 1, 3, 2]
-EARLY = [
-    ("fill", 0), ("fill", 1), ("fill", 2), ("fill", 3), ("fill", 4), ("fill", 5), ("fill", 6), ("fill", 7),
+FIRST = 0
+ORDER = [
+    ("hid", 0), ("fill", 6), ("fill", 2), ("hid", 2), ("hid", 6), ("fill", 1), ("turn", 0), ("routes", 0), ("raw", 0),
+    ("fill", 5), ("fill", 7), ("turn", 2), ("late", 0), ("row", 0), ("hid", 7), ("fill", 3), ("count", 0),
+    ("turn", 6), ("raw", 1), ("raw", 2), ("row", 2), ("raw", 3), ("hid", 3), ("far", 0), ("near", 0), ("relay", 0),
+    ("turn", 7), ("fill", 4), ("hid", 1), ("hid", 5), ("hid", 4), ("row", 6), ("far", 1), ("near", 1), ("far", 2),
+    ("row", 7), ("near", 2), ("far", 3), ("near", 3), ("turn", 3), ("relay", 6), ("relay", 2), ("relay", 7),
+    ("turn", 1), ("row", 3), ("turn", 5), ("pack", 0), ("turn", 4), ("row", 1), ("pack", 1), ("relay", 3), ("row", 5),
+    ("pack", 2), ("pack", 3, 0), ("row", 4), ("relay", 5), ("pack", 3, 1), ("relay", 1), ("mul", 0, 4, 8),
+    ("relay", 4), ("mul", 0, 0, 4), ("mul", 1, 0, 4), ("mul", 1, 4, 8), ("count", 1), ("mul", 2, 0, 4),
+    ("mul", 2, 4, 8), ("mul", 3, 0, 4, 0), ("mul", 3, 4, 8, 0), ("count", 2), ("mul", 3, 0, 4, 1),
+    ("mul", 3, 4, 8, 1),
 ]
-ORDER = [
-    ("hid", 0), ("hid", 5), ("turn", 0), ("routes", 0), ("hid", 4), ("hid", 6), ("turn", 5), ("late", 0), ("hid", 3),
-    ("row", 0), ("hid", 7), ("count", 0), ("hid", 2), ("row", 5), ("hid", 1), ("turn", 3), ("turn", 7), ("turn", 4),
-    ("raw", 1), ("relay", 0), ("raw", 0), ("turn", 6), ("raw", 3), ("row", 3), ("row", 6), ("turn", 2), ("turn", 1),
-    ("far", 0), ("raw", 2), ("row", 7), ("near", 0), ("relay", 6), ("pack", 0), ("far", 1), ("row", 1), ("near", 1),
-    ("far", 2), ("far", 3), ("row", 4), ("near", 2), ("row", 2), ("relay", 5), ("mul", 0, 0, 4), ("relay", 1),
-    ("near", 3), ("mul", 0, 4, 8), ("pack", 1), ("pack", 2), ("pack", 3), ("relay", 2), ("relay", 3), ("relay", 7),
-    ("relay", 4), ("mul", 1, 4, 8), ("count", 1), ("mul", 2, 4, 8), ("mul", 1, 0, 4), ("mul", 2, 0, 4), ("count", 2),
-    ("mul", 3, 0, 4), ("mul", 3, 4, 8),
-]
-
-
-def kernel(limit, total_pairs, hid_ref, ids_ref, weight_ref, og_ref, out_ref, load_ref,
-           meta_ref, pair_slot, graw, meta, gnear, gfar, gall, hp, hz, hzt, ht, acc, cnt, cnt_all, cnt_x,
-           s_send, s_meta, s_first, s_raw, s_gz, s_hz, s_hx, s_hy, s_cnt):
+
+
+def kernel(limit, total_pairs, hid_hbm, ids_hbm, weight_hbm, og_ref, out_ref, load_ref,
+           hid_ref, ids_ref, weight_ref, meta_ref, pair_slot, graw, meta, near_meta, gnear, gfar, gall, hp, hz, hzt, ht, acc, cnt, cnt_all, cnt_x,
+           s_send, s_meta, s_first, s_raw, s_gz, s_hz, s_hx, s_hy, s_cnt, s_own):
     cap, step = hp.shape[3], hp.shape[4]
     cols = graw.shape[5]
     toks = graw.shape[3] * graw.shape[4]
@@ -83,6 +83,15 @@
     partners += [owner(1, dz, dc)[2] for dz in (0, 1, 7, 2, 6) for dc in range(2)]
     for dev in partners:
         pl.semaphore_signal(barrier, inc=1, device_id=dev, device_id_type=MESH)
+
+    fetches = [
+        pltpu.make_async_copy(src, dst, s_own.at[i])
+        for i, (src, dst) in enumerate(((ids_hbm, ids_ref), (weight_hbm, weight_ref), (hid_hbm, hid_ref)))
+    ]
+    for fetch in fetches:
+        fetch.start()
+    for fetch in fetches[:2]:
+        fetch.wait()
 
     def across(ref, k):
         return jnp.concatenate([ref[m, k:k + 1, :] for m in range(micro)], axis=1)
@@ -134,15 +143,15 @@
             packed = jnp.dot(sel, rows_here, preferred_element_type=f32)
             hp[c, i] = packed.astype(bf16).reshape(NE, cap, step)
 
-    for name, *which in EARLY:
-        fill(*which)
+    fetches[2].wait()
+    fill(FIRST)
     pl.semaphore_wait(barrier, len(partners))
 
     toward = [(g, (NY - GROUP_DY[g]) % NY, dxl) for g in range(NY) for dxl in (1, 0)]
     for g, dy, dxl in toward:
         if dxl or dy:
-            send(meta_ref, meta.at[2, g * 2 + xlo], 0, s_meta.at[2], in_plane(dxl, dy)[2])
-    keep(meta_ref, meta.at[2, xlo], s_meta.at[2])
+            send(meta_ref, meta.at[g * 2 + xlo], 0, s_meta.at[2], in_plane(dxl, dy)[2])
+    keep(meta_ref, meta.at[xlo], s_meta.at[2])
 
     def first(g, dy, dxl):
         x2, y2, dev = in_plane(dxl, dy)
@@ -198,13 +207,15 @@
         send(ht.at[pl.ds(NX + 2, 2), c], ht.at[pl.ds(3 * NX + 2, 2), c], 7, s_hy.at[3, c], down)
 
     def routes(_):
-        wait(meta.at[2], s_meta.at[2])
+        wait(meta, s_meta.at[2])
+        for g in range(NY):
+            near_meta[2, g] = jnp.concatenate([meta[2 * g, 0:4, :], meta[2 * g + 1, 0:4, :]], axis=0)
+        total = meta[0, 4:5, :]
+        for q in range(1, 2 * NY):
+            total = total + meta[q, 4:5, :]
+        cnt[...] = total
         for dz, at in ((1, 1), (7, 3), (2, 0), (6, 4)):
-            send(meta.at[2], meta.at[at], 8, s_meta.at[at], zc(dz, 0)[1])
-        total = meta[2, 0]
-        for q in range(1, 2 * NY):
-            total = total + meta[2, q]
-        cnt[...] = total
+            send(near_meta.at[2], near_meta.at[at], 8, s_meta.at[at], zc(dz, 0)[1])
 
     plus, minus = zc(1, 0)[1], zc(7, 0)[1]
 
@@ -232,8 +243,8 @@
         last = s - chip_rows + h2 * half + z2 * (NC * cap)
         return jnp.where(r < chip_rows, near, jnp.where(s < chip_rows, beyond, last)).astype(jnp.float32)
 
-    def into_slots(g, sources):
-        @pl.loop(0, 2)
+    def into_slots(g, sources, xls):
+        @pl.loop(xls[0], xls[-1] + 1)
         def _(xl):
             for at in sources:
                 if at == 0:
@@ -242,7 +253,7 @@
                     rows = slots_of(chip_rows * 5 // 2, lax.rem(z + 7, NZ), 1 - xhi, lax.rem(z + 6, NZ))
                 else:
                     rows = slots_of(chip_rows, 0, 0, 0)
-                info = meta[at, g * 2 + xl]
+                info = jnp.where(xl == 0, near_meta[at, g, 0:4, :], near_meta[at, g, 4:8, :])
                 first = rows == info[0:1, :]
                 second = rows == info[1:2, :]
                 weights = jnp.where(first, info[2:3, :], jnp.where(second, info[3:4, :], 0.0))
@@ -254,12 +265,13 @@
                 if at == 0 or at == NEAR - 1:
                     gfar[g, at // 4, :, xl] = packed[chip_rows:].reshape(3 * NC, cap, cols)
 
-    def to_owners(g, first, count):
-        here, some = pl.ds(g * NX + xhi * 2, 2), pl.ds(first, count)
+    def to_owners(g, first, count, xls):
+        here, some = pl.ds(g * NX + xhi * 2 + xls[0], len(xls)), pl.ds(first, count)
+        from_xl, sem = pl.ds(xls[0], len(xls)), s_gz.at[g + (xls[0] if g == NY - 1 else 0)]
         for dxh, dc in ((1, 0), (1, 1), (0, 1)):
             d, _, dev = owner(dxh, 0, dc)
-            send(gnear.at[g, d, :, some], gall.at[here, core, some], 11, s_gz.at[g], dev)
-        keep(gnear.at[g, xhi * NC + core, :, some], gall.at[here, core, some], s_gz.at[g])
+            send(gnear.at[g, d, from_xl, some], gall.at[here, core, some], 11, sem, dev)
+        keep(gnear.at[g, xhi * NC + core, from_xl, some], gall.at[here, core, some], sem)
 
     seen = set()
 
@@ -267,30 +279,34 @@
         for at in offsets:
             if at not in seen:
                 seen.add(at)
-                wait(meta.at[at], s_meta.at[at])
+                wait(near_meta.at[at], s_meta.at[at])
 
     def near(g):
         known((1, 3))
-        into_slots(g, (1, 2, 3))
-        to_owners(g, 1, 3)
-
-    def pack(g):
+        into_slots(g, (1, 2, 3), (0, 1))
+        for xls in ((0, 1),) if g < NY - 1 else ((0,), (1,)):
+            to_owners(g, 1, 3, xls)
+
+    def pack(g, xl=0):
+        xls = (xl,) if g == NY - 1 else (0, 1)
         known((0, 4))
-        wait(graw.at[g, 0], s_raw.at[g, 0])
-        wait(graw.at[g, 4], s_raw.at[g, 4])
-        into_slots(g, (0, 4))
-        here = pl.ds(g * NX + xhi * 2, 2)
+        if xl == 0:
+            wait(graw.at[g, 0], s_raw.at[g, 0])
+            wait(graw.at[g, 4], s_raw.at[g, 4])
+        into_slots(g, (0, 4), xls)
+        here, from_xl = pl.ds(g * NX + xhi * 2 + xl, len(xls)), pl.ds(xl, len(xls))
+        sem = s_gz.at[g + xl]
         for side, dz, at in ((0, 1, 7), (1, 7, 5)):
             for dxh in range(2):
                 for dc in range(2):
                     d, _, dev = owner(dxh, dz, dc)
-                    send(gfar.at[g, side, d], gall.at[here, core, at], 10, s_gz.at[g], dev)
+                    send(gfar.at[g, side, d, from_xl], gall.at[here, core, at], 10, sem, dev)
         for side, dz in ((0, 2), (1, 6)):
             for dc in range(2):
                 _, c2, dev = owner(side, dz, dc)
-                send(gfar.at[g, side, 2 * NC + c2], gall.at[here, core, 6], 10, s_gz.at[g], dev)
-        to_owners(g, 0, 1)
-        to_owners(g, 4, 1)
+                send(gfar.at[g, side, 2 * NC + c2, from_xl], gall.at[here, core, 6], 10, sem, dev)
+        to_owners(g, 0, 1, xls)
+        to_owners(g, 4, 1, xls)
 
     def count(part):
         if part == 0:
@@ -310,41 +326,43 @@
 
     ready = set()
 
-    def mul(g, c0, c1):
-        if g not in ready:
-            ready.add(g)
-            wait(gall.at[pl.ds(g * NX, NX)], s_gz.at[g])
-        if g == NY - 1:
+    def mul(g, c0, c1, xl=None):
+        arrived = g if xl is None else g + xl
+        if arrived not in ready:
+            ready.add(arrived)
+            wait(gall.at[pl.ds(g * NX, NX if xl is None else 2)], s_gz.at[arrived])
+        if g == NY - 1 and xl == 0:
             for c in range(c0, c1):
                 wait(ht.at[pl.ds(3 * NX, 2), c], s_hy.at[2, c])
                 wait(ht.at[pl.ds(3 * NX + 2, 2), c], s_hy.at[3, c])
 
-        @pl.loop(c0, c1)
-        def _(c):
-            at = pl.ds(pl.multiple_of(c * step, step), step)
+        @pl.loop(c0 // 2, c1 // 2)
+        def _(pair):
+            two = pl.ds(pair * 2, 2)
+            at = pl.ds(pl.multiple_of(pair * 2 * step, 2 * step), 2 * step)
             part = None
-            for xs in range(NX):
+            for xs in range(NX) if xl is None else (xl, xl + 2):
                 q = g * NX + xs
-                term = jnp.dot(ht[q, c], gall[q].reshape(half, cols), preferred_element_type=jnp.float32)
+                term = jnp.dot(ht[q, two].reshape(2 * step, half), gall[q].reshape(half, cols), preferred_element_type=jnp.float32)
                 part = term if part is None else part + term
             if g == 0:
                 acc[at, :] = part
-            elif g < NY - 1:
+            elif g < NY - 1 or xl == 0:
                 acc[at, :] += part
             else:
                 out_ref[0, at, :] = (acc[at, :] + part).astype(out_ref.dtype)
 
-    steps = dict(late=late, near=near, count=count, hid=hid, routes=routes, raw=raw, turn=turn, far=far, row=row, relay=relay, pack=pack, mul=mul)
+    steps = dict(fill=fill, late=late, near=near, count=count, hid=hid, routes=routes, raw=raw, turn=turn, far=far, row=row, relay=relay, pack=pack, mul=mul)
     for name, *which in ORDER:
         steps[name](*which)
 
     wait(cnt_x.at[1], s_cnt.at[1])
-    load_ref[...] = ((cnt_x[0, 4:5, :] + cnt_x[1, 4:5, :]) / total_pairs)[0, :load_ref.shape[0]]
+    load_ref[...] = ((cnt_x[0] + cnt_x[1]) / total_pairs)[0, :load_ref.shape[0]]
 
     sent = (
-        meta.at[2, pl.ds(0, 7)], graw.at[0, 2, 0], graw.at[pl.ds(1, 3), 2], hz.at[:, :, :, pl.ds(0, 7)],
+        meta.at[pl.ds(0, 7)], graw.at[0, 2, 0], graw.at[pl.ds(1, 3), 2], hz.at[:, :, :, pl.ds(0, 7)],
         hz.at[:, :, 0, 0], ht.at[pl.ds(0, 3)], ht.at[pl.ds(0, 2 * NX)], ht.at[pl.ds(0, NX)],
-        meta.at[pl.ds(0, 4)], graw.at[:, pl.ds(0, 4)], gfar, gnear.at[:, pl.ds(0, 3)],
+        near_meta.at[pl.ds(0, 4)], graw.at[:, pl.ds(0, 4)], gfar, gnear.at[:, pl.ds(0, 3)],
         cnt_all.at[pl.ds(0, NE - 1)], cnt_x.at[0],
     )
     for i, ref in enumerate(sent):
@@ -369,13 +387,17 @@
             pltpu.VMEM((1, ff, cols), bf16),
             pltpu.VMEM((experts,), jnp.float32),
         ),
-        in_specs=[vmem, vmem, vmem, pl.BlockSpec(memory_space=pl.ANY)],
+        in_specs=[pl.BlockSpec(memory_space=pl.ANY)] * 4,
         out_specs=(vmem, vmem),
         scratch_shapes=[
+            pltpu.VMEM((micro, tokens, picks, ff), bf16),
+            pltpu.VMEM((micro, picks, tokens), jnp.int32),
+            pltpu.VMEM((micro, picks, tokens), jnp.float32),
             pltpu.VMEM((8, toks), jnp.float32),
             pltpu.VMEM((1, toks * picks), jnp.int32),
             pltpu.VMEM((NY, NEAR, 2, micro, tokens, cols), bf16),
-            pltpu.VMEM((NEAR, 2 * NY, 8, toks), jnp.float32),
+            pltpu.VMEM((2 * NY, 8, toks), jnp.float32),
+            pltpu.VMEM((NEAR, NY, 8, toks), jnp.float32),
             pltpu.VMEM((NY, 2 * NC, 2, NEAR, cap, cols), bf16),
             pltpu.VMEM((NY, 2, 3 * NC, 2, cap, cols), bf16),
             pltpu.VMEM((NQ, NC, NZ, cap, cols), bf16),
@@ -384,18 +406,19 @@
             pltpu.VMEM((CHUNKS, 2, ff // CHUNKS, NE * cap), bf16),
             pltpu.VMEM((NQ, CHUNKS, ff // CHUNKS, NE * cap), bf16),
             pltpu.VMEM((ff, cols), jnp.float32),
-            pltpu.VMEM((8, toks), jnp.float32),
-            pltpu.VMEM((NE, 8, toks), jnp.float32),
-            pltpu.VMEM((2, 8, toks), jnp.float32),
+            pltpu.VMEM((1, toks), jnp.float32),
+            pltpu.VMEM((NE, 1, toks), jnp.float32),
+            pltpu.VMEM((2, 1, toks), jnp.float32),
             dma((14,)),
             dma((NEAR,)),
             dma((NY,)),
             dma((NY, NEAR)),
-            dma((NY,)),
+            dma((NY + 1,)),
             dma((CHUNKS,)),
             dma((CHUNKS,)),
             dma((4, CHUNKS)),
             dma((2,)),
+            dma((3,)),
         ],
         compiler_params=pltpu.CompilerParams(
             collective_id=0, has_side_effects=True, vmem_limit_bytes=62_000_000 // 1024 * 1024

time: 194 us -> 186 us (0.959)
  Pallas kernels: 190 us -> 182 us
    pallas_call x1, Pallas kernels: 190 us -> 182 us  [body(): pl.pallas_call(functools.partial(kernel, limit, float(micro * tokens * re...]
where the time goes in v3:
time: 186 us; the launch traced here: 185 us
  Pallas kernels  182 us (98%)
  local copies, waits for them, and re-layouts  2.35 us (1%)
    pallas_call x1, Pallas kernels, body(): pl.pallas_call(functools.partial(kernel, limit, float(micro * tokens * re...  182 us

profile of v3, /device:TPU:1, one launch (start us, length us, event | category | flops | bytes accessed | tf_op | source)
XLA Modules:
  0.0 185.1 jit_solution(1821650730265653723)
XLA Ops:
  0.6 182.1 %shard_map.59 = (bf16[1,2048,896]{2,1,0:T(8,128)(2,1)S(1)}, f32[32]{0:T(128)S(1)}) custom-call(bf16[4,32,2,2048]{3,2,1,0:T(2,128)(2,1)} %hid_hbm.1, s32[4,2,32]{2,1,0:T(2,128)} %bitcast.2, f32[4,2,32]{2,1,0:T(2,128)} %bitcast.3, bf16[4,32,7168]{2,1,0:T(8,128)(2,1)} %og_ref.1), custom_call_target="tpu_custom_call" | custom-call | tf_op jit(solution)/shard_map/pallas_call | solution.py:384
  182.8 1.8 copy.8
  184.6 0.5 copy.9

commit v4 on v3

--- a/solution.py
+++ b/solution.py
@@ -21,16 +21,15 @@
 GROUP_DY = [0, 1, 3, 2]
 FIRST = 0
 ORDER = [
-    ("hid", 0), ("fill", 6), ("fill", 2), ("hid", 2), ("hid", 6), ("fill", 1), ("turn", 0), ("routes", 0), ("raw", 0),
-    ("fill", 5), ("fill", 7), ("turn", 2), ("late", 0), ("row", 0), ("hid", 7), ("fill", 3), ("count", 0),
-    ("turn", 6), ("raw", 1), ("raw", 2), ("row", 2), ("raw", 3), ("hid", 3), ("far", 0), ("near", 0), ("relay", 0),
-    ("turn", 7), ("fill", 4), ("hid", 1), ("hid", 5), ("hid", 4), ("row", 6), ("far", 1), ("near", 1), ("far", 2),
-    ("row", 7), ("near", 2), ("far", 3), ("near", 3), ("turn", 3), ("relay", 6), ("relay", 2), ("relay", 7),
-    ("turn", 1), ("row", 3), ("turn", 5), ("pack", 0), ("turn", 4), ("row", 1), ("pack", 1), ("relay", 3), ("row", 5),
-    ("pack", 2), ("pack", 3, 0), ("row", 4), ("relay", 5), ("pack", 3, 1), ("relay", 1), ("mul", 0, 4, 8),
-    ("relay", 4), ("mul", 0, 0, 4), ("mul", 1, 0, 4), ("mul", 1, 4, 8), ("count", 1), ("mul", 2, 0, 4),
-    ("mul", 2, 4, 8), ("mul", 3, 0, 4, 0), ("mul", 3, 4, 8, 0), ("count", 2), ("mul", 3, 0, 4, 1),
-    ("mul", 3, 4, 8, 1),
+    ("hid", 0), ("fill", 6), ("hid", 6), ("fill", 5), ("fill", 3), ("fill", 1), ("raw", 0), ("fill", 4), ("turn", 0),
+    ("hid", 1), ("turn", 6), ("late", 0), ("routes", 0), ("fill", 7), ("hid", 3), ("row", 0), ("far", 0), ("hid", 5),
+    ("row", 6), ("raw", 1), ("near", 0), ("count", 0), ("turn", 1), ("hid", 7), ("turn", 3), ("relay", 0), ("raw", 2),
+    ("fill", 2), ("raw", 3), ("pack", 0), ("hid", 4), ("relay", 6), ("row", 1), ("turn", 5), ("row", 3), ("hid", 2),
+    ("far", 1), ("near", 1), ("relay", 1), ("far", 2), ("near", 2), ("row", 5), ("turn", 7), ("far", 3), ("near", 3),
+    ("relay", 3), ("row", 7), ("turn", 4), ("turn", 2), ("relay", 5), ("row", 4), ("pack", 1), ("relay", 7),
+    ("pack", 2), ("row", 2), ("pack", 3, 0), ("relay", 4), ("mul", 0, 0, 4), ("mul", 0, 4, 8), ("mul", 1, 4, 8),
+    ("relay", 2), ("pack", 3, 1), ("mul", 1, 0, 4), ("count", 1), ("mul", 2, 4, 8), ("mul", 2, 0, 4),
+    ("mul", 3, 4, 8, 0), ("mul", 3, 0, 4, 0), ("count", 2), ("mul", 3, 0, 4, 1), ("mul", 3, 4, 8, 1),
 ]
 
 
@@ -336,14 +335,14 @@
                 wait(ht.at[pl.ds(3 * NX, 2), c], s_hy.at[2, c])
                 wait(ht.at[pl.ds(3 * NX + 2, 2), c], s_hy.at[3, c])
 
-        @pl.loop(c0 // 2, c1 // 2)
+        @pl.loop(c0 // 4, c1 // 4)
         def _(pair):
-            two = pl.ds(pair * 2, 2)
-            at = pl.ds(pl.multiple_of(pair * 2 * step, 2 * step), 2 * step)
+            two = pl.ds(pair * 4, 4)
+            at = pl.ds(pl.multiple_of(pair * 4 * step, 4 * step), 4 * step)
             part = None
             for xs in range(NX) if xl is None else (xl, xl + 2):
                 q = g * NX + xs
-                term = jnp.dot(ht[q, two].reshape(2 * step, half), gall[q].reshape(half, cols), preferred_element_type=jnp.float32)
+                term = jnp.dot(ht[q, two].reshape(4 * step, half), gall[q].reshape(half, cols), preferred_element_type=jnp.float32)
                 part = term if part is None else part + term
             if g == 0:
                 acc[at, :] = part

time: 186 us -> 185 us (level)
  no operation moved by 1% of the time
where the time goes in v4:
time: 185 us
  Pallas kernels  182 us (98%)
  local copies, waits for them, and re-layouts  2.35 us (1%)
    pallas_call x1, Pallas kernels, body(): pl.pallas_call(functools.partial(kernel, limit, float(micro * tokens * re...  182 us

profile of v4, /device:TPU:1, one launch (start us, length us, event | category | flops | bytes accessed | tf_op | source)
XLA Modules:
  0.0 184.7 jit_solution(7107987840582778916)
XLA Ops:
  0.6 181.7 %shard_map.59 = (bf16[1,2048,896]{2,1,0:T(8,128)(2,1)S(1)}, f32[32]{0:T(128)S(1)}) custom-call(bf16[4,32,2,2048]{3,2,1,0:T(2,128)(2,1)} %hid_hbm.1, s32[4,2,32]{2,1,0:T(2,128)} %bitcast.2, f32[4,2,32]{2,1,0:T(2,128)} %bitcast.3, bf16[4,32,7168]{2,1,0:T(8,128)(2,1)} %og_ref.1), custom_call_target="tpu_custom_call" | custom-call | tf_op jit(solution)/shard_map/pallas_call | solution.py:383
  182.4 1.8 copy.8
  184.2 0.5 copy.9

commit v5 on v4

--- a/solution.py
+++ b/solution.py
@@ -295,15 +295,15 @@
         into_slots(g, (0, 4), xls)
         here, from_xl = pl.ds(g * NX + xhi * 2 + xl, len(xls)), pl.ds(xl, len(xls))
         sem = s_gz.at[g + xl]
-        for side, dz, at in ((0, 1, 7), (1, 7, 5)):
-            for dxh in range(2):
-                for dc in range(2):
+        for dc in range(2):
+            for side, dz in ((0, 2), (1, 6)):
+                _, c2, dev = owner(side, dz, dc)
+                send(gfar.at[g, side, 2 * NC + c2, from_xl], gall.at[here, core, 6], 10, sem, dev)
+        for dxh in (1, 0):
+            for dc in range(2):
+                for side, dz, at in ((0, 1, 7), (1, 7, 5)):
                     d, _, dev = owner(dxh, dz, dc)
                     send(gfar.at[g, side, d, from_xl], gall.at[here, core, at], 10, sem, dev)
-        for side, dz in ((0, 2), (1, 6)):
-            for dc in range(2):
-                _, c2, dev = owner(side, dz, dc)
-                send(gfar.at[g, side, 2 * NC + c2, from_xl], gall.at[here, core, 6], 10, sem, dev)
         to_owners(g, 0, 1, xls)
         to_owners(g, 4, 1, xls)
 

time: 185 us -> 185 us (level)
  no operation moved by 1% of the time
where the time goes in v5:
time: 185 us
  Pallas kernels  182 us (98%)
  local copies, waits for them, and re-layouts  2.35 us (1%)
    pallas_call x1, Pallas kernels, body(): pl.pallas_call(functools.partial(kernel, limit, float(micro * tokens * re...  182 us

profile of v5, /device:TPU:1, one launch (start us, length us, event | category | flops | bytes accessed | tf_op | source)
XLA Modules:
  0.0 184.9 jit_solution(2781879841935755689)
XLA Ops:
  0.6 181.9 %shard_map.59 = (bf16[1,2048,896]{2,1,0:T(8,128)(2,1)S(1)}, f32[32]{0:T(128)S(1)}) custom-call(bf16[4,32,2,2048]{3,2,1,0:T(2,128)(2,1)} %hid_hbm.1, s32[4,2,32]{2,1,0:T(2,128)} %bitcast.2, f32[4,2,32]{2,1,0:T(2,128)} %bitcast.3, bf16[4,32,7168]{2,1,0:T(8,128)(2,1)} %og_ref.1), custom_call_target="tpu_custom_call" | custom-call | tf_op jit(solution)/shard_map/pallas_call | solution.py:383
  182.6 1.8 copy.8
  184.4 0.5 copy.9
